TPU v7x, 32 devices: a whole 2x2x4 slice. The times are simulated.
32 devices in a mesh: lon: 4 (over z), lat: 4 (over x, core), mem: 2 (over y).
Axes of the slice: x: 2, y: 2, z: 4, core: 2. Of those that a mesh axis runs over, the one named last changes fastest.
Arguments:
- tokens: bfloat16 [4, 8, 136, 24, 192], P('mem', None, 'lat', 'lon'), parts along dimension 0, may hold values from -6 to 6
- band_rows: int32 [4, 2], P('lat'), may hold values from 0 to 89, as said below
- down_gain: float32 [768], replicated, may hold values from 0.1 to 1.9
- down_shift: float32 [768], replicated, may hold values from -3 to 3
- down_weight: bfloat16 [768, 384], P(('lon', 'lat')), may hold values from -0.21875 to 0.21875
- up_weight: bfloat16 [384, 768], P(('lon', 'lat')), may hold values from -0.3125 to 0.3125
- up_gain: float32 [192], replicated, may hold values from 0.1 to 1.9
- up_shift: float32 [192], replicated, may hold values from -3 to 3
- mix_weight: bfloat16 [192, 192], replicated, may hold values from -0.4375 to 0.4375
Outputs:
- expanded: bfloat16 [4, 8, 136, 24, 192], P('mem', None, 'lat', 'lon'), parts along dimension 0
There are 2 independent parts, one for each index of `mem`. A program takes and returns all parts, laid end to end along the dimension named above; an argument that names none is the same for every part. Nothing has to cross between parts.
Inputs may be any that keep to these rules, and one draw needn't show every extreme that they name: `band_rows`: row b holds band b's first latitude row and one past its last; the bands cover rows 0 to 88 in order without gaps; band 0 holds an odd number of rows and every other band an even number; each band holds at least 2 * (5) rows and at most 34, and some band other than band 0 holds exactly 34.
All inputs are finite; a program needn't handle non-finite values.
Results may differ from a plain program's by a relative error of at most 0.0062.
Values may be sent and summed in bfloat16 or wider, within the bound.
A program may use at most 64 MiB of HBM per device.

v0:
```python
import jax
import jax.numpy as jnp
from jax import lax
from jax.sharding import PartitionSpec as P


def shifted(block, axis, distance):
    devices = range(lax.axis_size(axis))
    route = [((i - distance) % len(devices), i) for i in devices]
    return lax.ppermute(block, axis, route)


def passed_along(block, axis, distance):
    devices = range(lax.axis_size(axis))
    route = [(i - distance, i) for i in devices if i - distance in devices]
    return lax.ppermute(block, axis, route)


def normalize(values, scale_gain, bias_shift):
    average = jnp.mean(values, axis=-1, keepdims=True)
    centred = values - average
    spread = jnp.mean(centred * centred, axis=-1, keepdims=True)
    return centred * lax.rsqrt(spread + 1e-05) * scale_gain + bias_shift


def body(
    tokens, band_rows, down_gain, down_shift, down_weight, up_weight, up_gain, up_shift, mix_weight
):
    members, levels, slot_count, columns, features = tokens.shape
    half_rows = slot_count // 2 + 1
    first_row = band_rows[0, 0]
    live_rows = band_rows[0, 1] - first_row
    lat_odd = first_row % 2
    row_ids = lax.broadcasted_iota(jnp.int32, (1, 1, slot_count, 1, 1), 2)
    fields = jnp.where(row_ids < live_rows, tokens, jnp.zeros_like(tokens))
    right_col = shifted(fields[:, :, :, :1], "lon", -1)
    window = jnp.concatenate([fields[:, :, :, 1:], right_col], axis=3)
    window_cols = window.shape[3]
    half_cols = window_cols // 2
    next_first = passed_along(window[:, :, :1], "lat", -1)
    zero_rows = jnp.zeros((members, levels, 2, window_cols, features), window.dtype)
    extended = jnp.concatenate([window, zero_rows, zero_rows[:, :, :1]], axis=2)
    ext_ids = lax.broadcasted_iota(jnp.int32, (1, 1, slot_count + 3, 1, 1), 2)
    extended = jnp.where(ext_ids == live_rows, next_first, extended)
    patch_rows = lax.dynamic_slice_in_dim(extended, lat_odd, 2 * half_rows, 2)
    merged = patch_rows.reshape(members, levels, half_rows, 2, half_cols, 2, features)
    merged = merged.transpose(0, 1, 2, 4, 5, 3, 6).reshape(
        members * levels * half_rows * half_cols, 4 * features
    )
    merged_norm = normalize(merged.astype(jnp.float32), down_gain, down_shift).astype(jnp.bfloat16)
    columns_used = merged_norm
    coarse = jnp.dot(
        columns_used,
        lax.all_gather(down_weight, ("lon", "lat"), axis=0, tiled=True),
        preferred_element_type=jnp.float32,
    )
    coarse = coarse.astype(jnp.bfloat16)
    columns_used = coarse
    grown = jnp.dot(
        columns_used,
        lax.all_gather(up_weight, ("lon", "lat"), axis=0, tiled=True),
        preferred_element_type=jnp.float32,
    )
    grown = grown.reshape(members, levels, half_rows, half_cols, 2, 2, features)
    grown = grown.transpose(0, 1, 2, 4, 3, 5, 6).reshape(
        members, levels, 2 * half_rows, window_cols, features
    )
    fine_norm = normalize(grown, up_gain, up_shift).astype(jnp.bfloat16)
    fine_out = jnp.dot(
        fine_norm.reshape(-1, features), mix_weight, preferred_element_type=jnp.float32
    )
    fine_out = fine_out.astype(jnp.bfloat16).reshape(
        members, levels, 2 * half_rows, window_cols, features
    )
    overflow_row = lax.dynamic_slice_in_dim(fine_out, live_rows - lat_odd, 1, 2)
    from_above = passed_along(overflow_row, "lat", 1)
    padded_rows = jnp.concatenate([jnp.zeros_like(overflow_row), fine_out], axis=2)
    owned = lax.dynamic_slice_in_dim(padded_rows, 1 - lat_odd, slot_count, 2)
    owned = jnp.where((row_ids == 0) & (lat_odd == 1), from_above, owned)
    overflow_col = owned[:, :, :, columns - 1 :]
    from_left = shifted(overflow_col, "lon", 1)
    owned = jnp.concatenate([from_left, owned[:, :, :, : columns - 1]], axis=3)
    return jnp.where(row_ids < live_rows, owned, jnp.zeros_like(owned))


def solution(mesh):
    return jax.shard_map(
        body,
        mesh=mesh,
        in_specs=(
            P("mem", None, "lat", "lon", None),
            P("lat", None),
            P(),
            P(),
            P(("lon", "lat"), None),
            P(("lon", "lat"), None),
            P(),
            P(),
            P(),
        ),
        out_specs=P("mem", None, "lat", "lon", None),
        check_vma=False,
    )
```

profile of v0, /device:TPU:0, one launch (start us, length us, event | category | flops | bytes accessed | tf_op | source)
XLA Modules:
  0.0 134.9 jit_solution(14760807719825916473)
XLA Ops:
  0.0 0.0 copy-start
  0.0 1.3 fusion.16
  2.6 1.6 %broadcast_select_fusion = bf16[2,8,34,6,192]{4,1,3,2,0:T(8,128)(2,1)S(1)} fusion(bf16[2,8,34,6,192]{4,1,3,2,0:T(8,128)(2,1)} %param.9, pred[34]{0:T(512)(128)(4,1)S(1)} %iota_compare_fusion.1), kind=kLoop, calls=%fused_computation.21 | loop fusion | flops 626688 | bytes 2506786 | tf_op jit(solution)/shard_map/jit(_where)/select_n | solution.py:35
  4.2 0.0 copy-start.4
  4.2 0.7 slice.29
  5.0 5.1 %collective-permute-start = (bf16[2,8,34,1,192]{4,1,3,2,0:T(8,128)(2,1)}, bf16[2,8,34,1,192]{4,1,3,2,0:T(8,128)(2,1)S(1)}, u32[]{:S(2)}, u32[]{:S(2)}) collective-permute-start(bf16[2,8,34,1,192]{4,1,3,2,0:T(8,128)(2,1)} %slice.29), channel_id=1, source_target_pairs={{8,0},{16,8},{24,16},{0,24},{9,1},{17,9},{25,17},{1,25},{10,2},{18... | collective-permute-start | bytes 626696 | tf_op jit(solution)/shard_map/ppermute | solution.py:10
  11.9 0.1 slice.28
  12.0 0.0 copy-done.4
  12.0 22.9 %all_gather.6 = bf16[768,384]{1,0:T(8,128)(2,1)} all-gather(bf16[48,384]{1,0:T(8,128)(2,1)S(1)} %copy-done.4), channel_id=1, replica_groups=mesh['lon'=4,'lat'=4,'mem'=2] {'lon','lat'}, dimensions={0}, use_global_device_ids=true | all-gather | bytes 626688 | tf_op jit(solution)/shard_map/all_gather | solution.py:54
  35.0 0.0 copy-done.5
  35.0 20.4 %all_gather.7 = bf16[384,768]{1,0:T(8,128)(2,1)} all-gather(bf16[24,768]{1,0:T(8,128)(2,1)S(1)} %copy-done.5), channel_id=1, replica_groups=mesh['lon'=4,'lat'=4,'mem'=2] {'lon','lat'}, dimensions={0}, use_global_device_ids=true | all-gather | bytes 626688 | tf_op jit(solution)/shard_map/all_gather | solution.py:61
  55.4 0.0 collective-permute-done
  55.4 1.3 collective-permute-start.1
  56.7 0.1 pad_dynamic-slice_fusion.3
  56.8 0.1 pad.6.clone
  56.9 0.1 dynamic-slice.1
  57.0 0.1 dynamic-slice.2
  57.0 1.5 %collective-permute-done.1 = bf16[2,8,1,6,192]{4,1,3,2,0:T(8,128)(2,1)S(1)} collective-permute-done((bf16[2,8,1,6,192]{4,1,3,2,0:T(8,128)(2,1)S(1)}, bf16[2,8,1,6,192]{4,1,3,2,0:T(8,128)(2,1)S(1)}, u32[]{:S(2)}, u32[]{:S(2)}) %collective-permute-start.1) | collective-permute-done | bytes 36896 | tf_op jit(solution)/shard_map/ppermute | solution.py:16
  58.5 0.0 copy-start.3
  58.5 0.6 copy-done.3
  59.2 1.4 %fusion.3 = bf16[2,8,36,6,192]{4,1,3,2,0:T(8,128)(2,1)S(1)} fusion(s32[]{:T(128)S(6)} %select_n.34, bf16[2,8,34,5,192]{4,1,3,2,0:T(8,128)(2,1)S(1)} %slice.28, bf16[2,8,34,1,192]{4,1,3,2,0:T(8,128)(2,1)S(1)} %collective-permute-done, pred[36]{0:T(512)(128)(4,1)S(1)} %dynamic-slice.2, bf16[2,8,6,192]{3,1,2,0:T(8,128)(2,1)} %bitcast.30, ...), kind=kLoop, calls=%fused_computation.13 | loop fusion | flops 2654208 | bytes 2617528 | tf_op jit(solution)/shard_map/jit(_where)/select_n | solution.py:44
  60.6 0.4 fusion.4
  61.0 0.1 copy.33
  61.1 0.1 copy.35
  61.2 0.2 copy.34
  61.4 2.3 %convert_bitcast_fusion = f32[2,8,18,3,2,2,192]{6,1,4,3,5,2,0:T(8,128)} fusion(bf16[2,8,18,2,3,2,192]{6,1,5,4,3,2,0:T(8,128)(2,1)S(1)} %bitcast.26), kind=kLoop, calls=%fused_computation.1 | loop fusion | flops 663552 | bytes 3981312 | tf_op jit(solution)/shard_map/convert_element_type | solution.py:50
  63.7 0.7 multiply_reduce_fusion.1
  64.4 0.1 copy.36
  64.5 0.2 copy.37
  64.7 0.2 rsqrt.23
  64.9 0.2 div.17
  65.1 6.5 %copy.32 = f32[2,8,18,3,2,2,192]{6,5,4,3,2,1,0:T(2,128)} copy(f32[2,8,18,3,2,2,192]{6,1,4,3,5,2,0:T(8,128)} %convert_bitcast_fusion) | data formatting | bytes 5308416 | tf_op jit(solution)/shard_map/convert_element_type | solution.py:50
  71.7 0.0 copy-start.2
  71.7 0.0 copy-start.8
  71.7 4.8 %reshape.108 = f32[864,768]{1,0:T(8,128)S(1)} reshape(f32[2,8,18,3,2,2,192]{6,5,4,3,2,1,0:T(2,128)} %copy.32) | data formatting | bytes 5308416 | tf_op jit(solution)/shard_map/convert_element_type | solution.py:50
  76.5 0.0 copy-done.2
  76.5 0.0 copy-done.8
  76.5 0.0 copy-done.9
  76.5 4.4 %fusion.14 = f32[864,768]{1,0:T(8,128)} fusion(bf16[384,768]{1,0:T(8,128)(2,1)} %all_gather.7, bf16[768,384]{1,0:T(8,128)(2,1)S(1)} %copy-done.2, f32[864,768]{1,0:T(8,128)S(1)} %reshape.108, f32[768]{0:T(1024)S(1)} %copy-done.8, f32[768]{0:T(1024)S(1)} %copy-done.9, f32[864]{0:T(1024)S(1)} %rsqrt.23, f32[864]{0:T(1024)S(1)} %div.17), kind=kOutput, calls=%fused_computation.27 | convolution fusion | flops 1022865408 | bytes 6501120 | tf_op jit(solution)/shard_map/dot_general | solution.py:59
  80.9 6.3 %reshape.105 = f32[2,8,18,3,2,2,192]{6,5,4,3,2,1,0:T(2,128)} reshape(f32[864,768]{1,0:T(8,128)} %fusion.14) | data formatting | bytes 5308416 | tf_op jit(solution)/shard_map/reshape | solution.py:64
  87.2 4.2 %fusion.15 = f32[2,8,18,2,3,2]{5,4,3,2,1,0:T(4,128)S(1)} fusion(f32[2,8,18,3,2,2,192]{6,5,4,3,2,1,0:T(2,128)} %reshape.105), kind=kLoop, calls=%fused_computation.39 | loop fusion | flops 660096 | bytes 2668032 | tf_op jit(solution)/shard_map/reduce_sum | solution.py:20
  91.5 0.3 broadcast_multiply_fusion
  91.8 0.6 div.20
  92.4 0.0 copy-start.1
  92.4 5.9 %multiply_reduce_fusion = f32[2,8,18,2,3,2]{5,4,3,2,1,0:T(4,128)S(1)} fusion(f32[2,8,18,2,3,2]{5,4,3,2,1,0:T(4,128)S(1)} %broadcast_multiply_fusion, f32[2,8,18,3,2,2,192]{6,5,4,3,2,1,0:T(2,128)} %reshape.105), kind=kLoop, calls=%fused_computation.4 | loop fusion | flops 1987200 | bytes 2681856 | tf_op jit(solution)/shard_map/reduce_sum | solution.py:22
  98.3 0.0 copy-done.1
  98.3 3.0 %copy.48 = f32[2,8,18,3,2,2,192]{6,5,3,4,2,1,0:T(2,128)} copy(f32[2,8,18,3,2,2,192]{6,5,4,3,2,1,0:T(2,128)S(1)} %copy-done.1) | data formatting | bytes 5308416 | tf_op jit(solution)/shard_map/reshape | solution.py:64
  101.3 5.4 %reshape.106 = f32[3456,192]{1,0:T(8,128)} reshape(f32[2,8,18,2,3,2,192]{6,5,4,3,2,1,0:T(2,128)} %bitcast.28) | data formatting | bytes 5308416 | tf_op jit(solution)/shard_map/reshape | solution.py:65
  106.7 0.4 add_rsqrt_fusion
  107.1 0.6 rsqrt.25
  107.7 0.0 copy-done
  107.7 0.0 copy-done.6
  107.7 0.0 copy-done.7
  107.7 3.3 %convolution_convert_fusion = bf16[3456,192]{0,1:T(8,128)(2,1)S(1)} fusion(bf16[192,192]{1,0:T(8,128)(2,1)S(1)} %copy-done, f32[3456,192]{1,0:T(8,128)} %reshape.106, f32[192]{0:T(256)S(1)} %copy-done.6, f32[192]{0:T(256)S(1)} %copy-done.7, f32[3456]{0:T(1024)S(1)} %rsqrt.25, f32[3456]{0:T(1024)S(1)} %div.20), kind=kOutput, calls=%fused_computation | convolution fusion | flops 258785280 | bytes 4084224 | tf_op jit(solution)/shard_map/dot_general | solution.py:69
  111.0 2.2 %copy.39 = bf16[3456,192]{1,0:T(8,128)(2,1)} copy(bf16[3456,192]{0,1:T(8,128)(2,1)S(1)} %convolution_convert_fusion) | data formatting | bytes 2654208 | tf_op jit(solution)/shard_map/convert_element_type | solution.py:72
  113.2 2.8 %reshape.107 = bf16[2,8,36,6,192]{4,3,2,1,0:T(8,128)(2,1)S(1)} reshape(bf16[3456,192]{1,0:T(8,128)(2,1)} %copy.39) | data formatting | bytes 2654208 | tf_op jit(solution)/shard_map/reshape | solution.py:72
  116.1 4.5 %collective-permute-start.2 = (bf16[2,8,1,6,192]{4,3,2,1,0:T(8,128)(2,1)S(1)}, bf16[2,8,1,6,192]{4,3,2,1,0:T(8,128)(2,1)S(1)}, u32[]{:S(2)}, u32[]{:S(2)}) collective-permute-start(bf16[2,8,1,6,192]{4,3,2,1,0:T(8,128)(2,1)S(1)} %constant_dynamic-slice_fusion), channel_id=1, source_target_pairs={{0,2},{2,4},{4,6},{1,3},{3,5},{5,7},{8,10},{10,12},{12,14},{9,11},... | collective-permute-start | bytes 110600 | tf_op jit(solution)/shard_map/ppermute | solution.py:16
  120.6 1.9 %copy.41 = bf16[2,8,36,6,192]{4,1,3,2,0:T(8,128)(2,1)S(1)} copy(bf16[2,8,36,6,192]{4,3,2,1,0:T(8,128)(2,1)S(1)} %reshape.107) | data formatting | bytes 2654208 | tf_op jit(solution)/shard_map/reshape | solution.py:72
  122.5 0.0 collective-permute-done.2
  122.6 0.3 fusion.9
  122.9 0.1 collective-permute-start.3
  123.0 0.1 slice.31
  123.1 10.3 %collective-permute-done.3 = bf16[2,8,34,1,192]{4,1,3,2,0:T(8,128)(2,1)S(1)} collective-permute-done((bf16[2,8,34,1,192]{4,1,3,2,0:T(8,128)(2,1)S(1)}, bf16[2,8,34,1,192]{4,1,3,2,0:T(8,128)(2,1)S(1)}, u32[]{:S(2)}, u32[]{:S(2)}) %collective-permute-start.3) | collective-permute-done | bytes 208928 | tf_op jit(solution)/shard_map/ppermute | solution.py:10
  133.3 1.5 %maximum_select_fusion = bf16[2,8,34,6,192]{4,1,3,2,0:T(8,128)(2,1)} fusion(bf16[2,8,34,5,192]{4,1,3,2,0:T(8,128)(2,1)S(1)} %slice.31, bf16[2,8,34,1,192]{4,1,3,2,0:T(8,128)(2,1)S(1)} %collective-permute-done.3, pred[34]{0:T(512)(128)(4,1)S(1)} %iota_compare_fusion.1), kind=kLoop, calls=%fused_computation.20 | loop fusion | flops 1253376 | bytes 2506786 | tf_op jit(solution)/shard_map/jit(_where)/select_n | solution.py:83
  (14 shorter events, 0.1 us)
Async XLA Ops:
  0.0 107.7 %copy-start = (bf16[192,192]{1,0:T(8,128)(2,1)S(1)}, bf16[192,192]{1,0:T(8,128)(2,1)}, u32[]{:S(2)}) copy-start(bf16[192,192]{1,0:T(8,128)(2,1)} %param.17) | copy-start | bytes 221188
  4.2 7.8 %copy-start.4 = (bf16[48,384]{1,0:T(8,128)(2,1)S(1)}, bf16[48,384]{1,0:T(8,128)(2,1)}, u32[]{:S(2)}) copy-start(bf16[48,384]{1,0:T(8,128)(2,1)} %param.13) | copy-start | bytes 110596
  5.0 30.0 %copy-start.5 = (bf16[24,768]{1,0:T(8,128)(2,1)S(1)}, bf16[24,768]{1,0:T(8,128)(2,1)}, u32[]{:S(2)}) copy-start(bf16[24,768]{1,0:T(8,128)(2,1)} %param.14) | copy-start | bytes 110596
  5.0 50.4 %collective-permute-start = (bf16[2,8,34,1,192]{4,1,3,2,0:T(8,128)(2,1)}, bf16[2,8,34,1,192]{4,1,3,2,0:T(8,128)(2,1)S(1)}, u32[]{:S(2)}, u32[]{:S(2)}) collective-permute-start(bf16[2,8,34,1,192]{4,1,3,2,0:T(8,128)(2,1)} %slice.29), channel_id=1, source_target_pairs={{8,0},{16,8},{24,16},{0,24},{9,1},{17,9},{25,17},{1,25},{10,2},{18... | collective-permute-start | bytes 626696 | tf_op jit(solution)/shard_map/ppermute | solution.py:10
  55.4 3.1 %collective-permute-start.1 = (bf16[2,8,1,6,192]{4,1,3,2,0:T(8,128)(2,1)S(1)}, bf16[2,8,1,6,192]{4,1,3,2,0:T(8,128)(2,1)S(1)}, u32[]{:S(2)}, u32[]{:S(2)}) collective-permute-start(bf16[2,8,1,6,192]{4,1,3,2,0:T(8,128)(2,1)S(1)} %pad_maximum_fusion), channel_id=1, source_target_pairs={{2,0},{4,2},{6,4},{3,1},{5,3},{7,5},{10,8},{12,10},{14,12},{11,9},... | collective-permute-start | bytes 110600 | tf_op jit(solution)/shard_map/ppermute | solution.py:16
  58.5 0.6 copy-start.3
  71.7 4.8 %copy-start.2 = (bf16[768,384]{1,0:T(8,128)(2,1)S(1)}, bf16[768,384]{1,0:T(8,128)(2,1)}, u32[]{:S(2)}) copy-start(bf16[768,384]{1,0:T(8,128)(2,1)} %all_gather.6) | copy-start | bytes 1769476
  71.7 4.9 %copy-start.8 = (f32[768]{0:T(1024)S(1)}, f32[768]{0:T(1024)}, u32[]{:S(2)}) copy-start(f32[768]{0:T(1024)} %param.12) | copy-start | bytes 9220
  71.7 4.9 %copy-start.9 = (f32[768]{0:T(1024)S(1)}, f32[768]{0:T(1024)}, u32[]{:S(2)}) copy-start(f32[768]{0:T(1024)} %param.11) | copy-start | bytes 9220
  92.4 5.9 %copy-start.1 = (f32[2,8,18,3,2,2,192]{6,5,4,3,2,1,0:T(2,128)S(1)}, f32[2,8,18,3,2,2,192]{6,5,4,3,2,1,0:T(2,128)}, u32[]{:S(2)}) copy-start(f32[2,8,18,3,2,2,192]{6,5,4,3,2,1,0:T(2,128)} %reshape.105) | copy-start | bytes 7962628
  106.7 1.0 copy-start.6
  106.7 1.0 copy-start.7
  116.1 6.5 %collective-permute-start.2 = (bf16[2,8,1,6,192]{4,3,2,1,0:T(8,128)(2,1)S(1)}, bf16[2,8,1,6,192]{4,3,2,1,0:T(8,128)(2,1)S(1)}, u32[]{:S(2)}, u32[]{:S(2)}) collective-permute-start(bf16[2,8,1,6,192]{4,3,2,1,0:T(8,128)(2,1)S(1)} %constant_dynamic-slice_fusion), channel_id=1, source_target_pairs={{0,2},{2,4},{4,6},{1,3},{3,5},{5,7},{8,10},{10,12},{12,14},{9,11},... | collective-permute-start | bytes 110600 | tf_op jit(solution)/shard_map/ppermute | solution.py:16
  122.9 10.4 %collective-permute-start.3 = (bf16[2,8,34,1,192]{4,1,3,2,0:T(8,128)(2,1)S(1)}, bf16[2,8,34,1,192]{4,1,3,2,0:T(8,128)(2,1)S(1)}, u32[]{:S(2)}, u32[]{:S(2)}) collective-permute-start(bf16[2,8,34,1,192]{4,1,3,2,0:T(8,128)(2,1)S(1)} %slice.30), channel_id=1, source_target_pairs={{24,0},{0,8},{8,16},{16,24},{25,1},{1,9},{9,17},{17,25},{26,2},{2,... | collective-permute-start | bytes 626696 | tf_op jit(solution)/shard_map/ppermute | solution.py:10
where the time goes:
time: 136 us; the launch traced here: 135 us
  blocking collectives  43.4 us (32%)
  local copies, waits for them, and re-layouts  38.6 us (28%)
  other arithmetic  19.2 us (14%)
  waiting for transfers between devices  11.8 us (9%)
  starting transfers between devices  11 us (8%)
  matrix products  7.64 us (6%)
  between operations  3.41 us (3%)
    all_gather x1, blocking collectives, body(): lax.all_gather(down_weight, ('lon', 'lat'), axis=0, tiled=True)  22.9 us
    all_gather x1, blocking collectives, body(): lax.all_gather(up_weight, ('lon', 'lat'), axis=0, tiled=True)  20.4 us
    convert_element_type x2, local copies, waits for them, and re-layouts, body(): merged.astype(jnp.float32)  11.4 us
    ppermute x2, waiting for transfers between devices, shifted(): return lax.ppermute(block, axis, route)  10.3 us
    reshape x2, local copies, waits for them, and re-layouts, body(): grown = grown.reshape(members, levels, half_rows, half_cols, 2, 2, features)  9.24 us
    reduce_sum x2, other arithmetic, normalize(): spread = jnp.mean(centred * centred, axis=-1, keepdims=True)  6.61 us
    ppermute x2, starting transfers between devices, passed_along(): return lax.ppermute(block, axis, route)  5.84 us
    reshape x1, local copies, waits for them, and re-layouts, body(): grown.transpose(0, 1, 2, 4, 3, 5, 6)  5.4 us
  transfers between devices with their start and end apart: 4, of which 2 were waited for; matrix products, arithmetic and copies ran while one was open for 2% of the time, Pallas kernels for 0%

commit v1 on v0

v1 whole, which is shorter than its diff:
```python
import functools

import jax
import jax.numpy as jnp
from jax import lax
from jax.experimental import pallas as pl
from jax.experimental.pallas import tpu as pltpu
from jax.sharding import PartitionSpec as P

LANES = 128
SUBLANES = 8


def shifted(block, axis, distance):
    devices = range(lax.axis_size(axis))
    route = [((i - distance) % len(devices), i) for i in devices]
    return lax.ppermute(block, axis, route)


def passed_along(block, axis, distance):
    devices = range(lax.axis_size(axis))
    route = [(i - distance, i) for i in devices if i - distance in devices]
    return lax.ppermute(block, axis, route)


def normalized(planes, gains, shifts, width):
    total = functools.reduce(jnp.add, planes)
    average = jnp.sum(total, axis=-1, keepdims=True) * (1.0 / width)
    centred = [plane - average for plane in planes]
    squares = functools.reduce(jnp.add, [c * c for c in centred])
    spread = jnp.sum(squares, axis=-1, keepdims=True) * (1.0 / width)
    scale = lax.rsqrt(spread + 1e-05)
    return [
        (c * scale * gain + shift).astype(jnp.bfloat16)
        for c, gain, shift in zip(centred, gains, shifts)
    ]


def compute_kernel(
    band_ref, tokens_ref, west_ref, east_ref, north_ref, south_ref,
    down_gain_ref, down_shift_ref, down_weight_ref, up_weight_ref,
    up_gain_ref, up_shift_ref, mix_ref, out_ref, low_ref, high_ref, side_low, side_high,
):
    units, slots, columns, features = tokens_ref.shape
    pitch = -(-(columns + 2) // SUBLANES) * SUBLANES
    half_pitch = pitch // 2
    half_rows = slots // 2 + 1
    plane_rows = low_ref.shape[1] // 2
    patches = half_rows * half_pitch
    rest = features - LANES
    first_row = band_ref[0, 0]
    live = band_ref[0, 1] - first_row
    odd = lax.rem(first_row, 2)

    def cell(row):
        moved = row + odd
        at = lax.rem(moved, 2) * plane_rows + SUBLANES + pitch * (moved // 2)
        return pl.multiple_of(at, SUBLANES)

    def put(unit, at, count, values):
        low_ref[unit, pl.ds(at, count), :] = values[:, :LANES]
        high_ref[unit, pl.ds(at, count), :rest] = values[:, LANES:]

    def fill(unit, carry):
        for row in range(slots):
            put(unit, cell(row), columns, tokens_ref[unit, row].astype(jnp.float32))
        for side_ref, offset in ((west_ref, -1), (east_ref, columns)):
            side = side_ref[unit].astype(jnp.float32)
            side_low[...] = side[:, :LANES]
            side_high[:, :rest] = side[:, LANES:]
            for parity in range(2):
                at = cell(parity) + offset
                reads = pl.ds(parity, slots // 2, stride=2)
                writes = pl.ds(at, slots // 2, stride=pitch)
                low_ref[unit, writes, :] = side_low[reads, :]
                high_ref[unit, writes, :] = side_high[reads, :]

        def whole_row(values, row):
            at = cell(row)
            put(unit, at, columns + 1, values[: columns + 1])
            put(unit, at - 1, 1, values[columns + 1 : columns + 2])

        @pl.when(odd == 1)
        def _():
            whole_row(north_ref[unit].astype(jnp.float32), -1)

        whole_row(south_ref[unit].astype(jnp.float32), live)
        return carry

    lax.fori_loop(0, units, fill, 0)

    def plane(p, q):
        reads = pl.ds(p * plane_rows + SUBLANES - 1 + q, patches, stride=2)
        lows = [low_ref[unit, reads, :] for unit in range(units)]
        highs = [high_ref[unit, reads, :][:, :rest] for unit in range(units)]
        return jnp.concatenate([jnp.concatenate(lows, 0), jnp.concatenate(highs, 0)], 1)

    order = [(p, q) for q in range(2) for p in range(2)]
    gains = [down_gain_ref[i : i + 1] for i in range(4)]
    shifts = [down_shift_ref[i : i + 1] for i in range(4)]
    merged = normalized([plane(p, q) for p, q in order], gains, shifts, 4 * features)
    coarse = functools.reduce(
        jnp.add,
        [
            jnp.dot(
                part,
                down_weight_ref[i * features : (i + 1) * features],
                preferred_element_type=jnp.float32,
            )
            for i, part in enumerate(merged)
        ],
    ).astype(jnp.bfloat16)
    for i, (p, q) in enumerate((p, q) for p in range(2) for q in range(2)):
        grown = jnp.dot(
            coarse,
            up_weight_ref[:, i * features : (i + 1) * features],
            preferred_element_type=jnp.float32,
        )
        (fine,) = normalized([grown], [up_gain_ref[...]], [up_shift_ref[...]], features)
        fine_out = jnp.dot(fine, mix_ref[...], preferred_element_type=jnp.float32)
        writes = pl.ds(p * plane_rows + SUBLANES - 1 + q, patches, stride=2)
        for unit in range(units):
            piece = fine_out[unit * patches : (unit + 1) * patches]
            low_ref[unit, writes, :] = piece[:, :LANES]
            high_ref[unit, writes, :] = jnp.concatenate(
                [piece[:, LANES:], piece[:, LANES:]], 1
            ) if rest * 2 == LANES else jnp.pad(piece[:, LANES:], ((0, 0), (0, LANES - rest)))

    def drain(unit, carry):
        for row in range(slots):
            at = cell(row)
            values = jnp.concatenate(
                [low_ref[unit, pl.ds(at, columns), :], high_ref[unit, pl.ds(at, columns), :rest]], 1
            )
            values = jnp.where(row < live, values, jnp.zeros_like(values))
            out_ref[unit, row] = values.astype(jnp.bfloat16)
        return carry

    lax.fori_loop(0, units, drain, 0)


def compute(tokens, band_rows, sides, norms, weights, block=4):
    units, slots, columns, features = tokens.shape
    pitch = -(-(columns + 2) // SUBLANES) * SUBLANES
    plane_rows = SUBLANES + pitch * (slots // 2 + 1)
    down_gain, down_shift, up_gain, up_shift = norms

    def per_unit(*shape):
        return pl.BlockSpec((block, *shape), lambda i: (i,) + (0,) * len(shape))

    def whole(array):
        return pl.BlockSpec(array.shape, lambda i: (0,) * array.ndim)

    params = [
        down_gain.reshape(4, features), down_shift.reshape(4, features), weights[0], weights[1],
        up_gain.reshape(1, features), up_shift.reshape(1, features), weights[2],
    ]
    return pl.pallas_call(
        compute_kernel,
        grid=(units // block,),
        out_shape=jax.ShapeDtypeStruct(tokens.shape, tokens.dtype),
        in_specs=[
            pl.BlockSpec(memory_space=pltpu.SMEM),
            per_unit(slots, columns, features),
            per_unit(slots, features),
            per_unit(slots, features),
            per_unit(columns + 2, features),
            per_unit(columns + 2, features),
            *[whole(p) for p in params],
        ],
        out_specs=per_unit(slots, columns, features),
        scratch_shapes=[
            pltpu.VMEM((block, 2 * plane_rows, LANES), jnp.float32),
            pltpu.VMEM((block, 2 * plane_rows, LANES), jnp.float32),
            pltpu.VMEM((slots, LANES), jnp.float32),
            pltpu.VMEM((slots, LANES), jnp.float32),
        ],
        compiler_params=pltpu.CompilerParams(dimension_semantics=("arbitrary",)),
        cost_estimate=pl.CostEstimate(
            flops=3_000_000_000, bytes_accessed=8_000_000, transcendentals=0
        ),
    )(band_rows, tokens, *sides, *params)


def body(
    tokens, band_rows, down_gain, down_shift, down_weight, up_weight, up_gain, up_shift, mix_weight
):
    members, levels, slots, columns, features = tokens.shape
    units = members * levels
    flat = tokens.reshape(units, slots, columns, features)
    live = band_rows[0, 1] - band_rows[0, 0]
    west = shifted(flat[:, :, columns - 1], "lon", 1)
    east = shifted(flat[:, :, 0], "lon", -1)

    def with_sides(row):
        pick = lambda array: lax.dynamic_slice_in_dim(array, row, 1, 1)
        return jnp.concatenate([pick(flat)[:, 0], pick(east), pick(west)], axis=1)

    north = passed_along(with_sides(live - 1), "lat", 1)
    south = passed_along(with_sides(0), "lat", -1)
    down = lax.all_gather(down_weight, ("lon", "lat"), axis=0, tiled=True)
    up = lax.all_gather(up_weight, ("lon", "lat"), axis=0, tiled=True)
    out = compute(
        flat, band_rows, (west, east, north, south),
        (down_gain, down_shift, up_gain, up_shift), (down, up, mix_weight),
    )
    return out.reshape(tokens.shape)


def solution(mesh):
    return jax.shard_map(
        body,
        mesh=mesh,
        in_specs=(
            P("mem", None, "lat", "lon", None),
            P("lat", None),
            P(),
            P(),
            P(("lon", "lat"), None),
            P(("lon", "lat"), None),
            P(),
            P(),
            P(),
        ),
        out_specs=P("mem", None, "lat", "lon", None),
        check_vma=False,
    )
```

time: 136 us -> 92.1 us (0.68)
  local copies, waits for them, and re-layouts: 38.6 us -> 11.1 us
  other arithmetic: 19.2 us -> 0.13 us
  Pallas kernels: 0 us -> 17.3 us
  waiting for transfers between devices: 11.8 us -> 0.01 us
  blocking collectives: 43.4 us -> 52.5 us
  matrix products: 7.64 us -> 0 us
  between operations: 3.41 us -> 1.34 us
  starting transfers between devices: 11 us -> 9.46 us
    pallas_call x0 -> x1, Pallas kernels: none -> 17.3 us  [compute(): pl.pallas_call(compute_kernel, grid=(units // block,), out_shape=jax.Shap...]
    convert_element_type x3 -> x0, local copies, waits for them, and re-layouts: 13.6 us -> none  [the longest x2 11.4 us: body(): merged.astype(jnp.float32)]
    reshape x5 -> x4, local copies, waits for them, and re-layouts: 19.4 us -> 7.42 us  [the longest x1 3.75 us: body(): return out.reshape(tokens.shape)]
    reduce_sum x4 -> x0, other arithmetic: 11.3 us -> none  [the longest x2 6.61 us: normalize(): spread = jnp.mean(centred * centred, axis=-1, keepdims=True)]
    ppermute x2, waiting for transfers between devices: 10.3 us -> 0.01 us  [shifted(): return lax.ppermute(block, axis, route)]
    all_gather x2, blocking collectives: 43.4 us -> 52.5 us  [the longest x1 30.8 us: body(): down = lax.all_gather(down_weight, ('lon', 'lat'), axis=0, tiled=True)]
    dot_general x2 -> x0, matrix products: 7.64 us -> none  [the longest x1 4.37 us: body(): jnp.dot(columns_used, lax.all_gather(up_weight, ('lon', 'lat'), axis=0, t...]
    select_n x4 -> x0, other arithmetic: 4.86 us -> none  [the longest x1 1.62 us: body(): fields = jnp.where(row_ids < live_rows, tokens, jnp.zeros_like(tokens))]
  transfers between devices with their start and end apart: 4 -> 4, of which waited for: 2 -> 0; matrix products, arithmetic and copies ran while one was open for 2% -> 5% of each run, Pallas kernels for 0% -> 0%
where the time goes in v1:
time: 92.1 us; the launch traced here: 91.8 us
  blocking collectives  52.5 us (57%)
  Pallas kernels  17.3 us (19%)
  local copies, waits for them, and re-layouts  11.1 us (12%)
  starting transfers between devices  9.46 us (10%)
  between operations  1.34 us (1%)
    all_gather x1, blocking collectives, body(): down = lax.all_gather(down_weight, ('lon', 'lat'), axis=0, tiled=True)  30.8 us
    all_gather x1, blocking collectives, body(): up = lax.all_gather(up_weight, ('lon', 'lat'), axis=0, tiled=True)  21.7 us
    pallas_call x1, Pallas kernels, compute(): pl.pallas_call(compute_kernel, grid=(units // block,), out_shape=jax.Shap...  17.3 us
    ppermute x2, starting transfers between devices, shifted(): return lax.ppermute(block, axis, route)  5.13 us
    ppermute x2, starting transfers between devices, passed_along(): return lax.ppermute(block, axis, route)  4.33 us
    reshape x1, local copies, waits for them, and re-layouts, body(): return out.reshape(tokens.shape)  3.75 us
    unnamed x19, local copies, waits for them, and re-layouts  2.72 us
    reshape x1, local copies, waits for them, and re-layouts, body(): flat = tokens.reshape(units, slots, columns, features)  2.35 us
  transfers between devices with their start and end apart: 4, of which 0 were waited for; matrix products, arithmetic and copies ran while one was open for 5% of the time, Pallas kernels for 0%

profile of v1, /device:TPU:0, one launch (start us, length us, event | category | flops | bytes accessed | tf_op | source)
XLA Modules:
  0.0 91.8 jit_solution(13653359757699124977)
XLA Ops:
  0.0 0.0 copy-start.6
  0.0 0.0 copy-start
  0.0 2.1 %copy.14 = bf16[2,8,34,6,192]{4,2,1,0,3:T(8,128)(2,1)S(1)} copy(bf16[2,8,34,6,192]{4,1,3,2,0:T(8,128)(2,1)} %param.9) | data formatting | bytes 2506752 | tf_op args[0]
  2.1 0.0 copy-start.1
  2.1 5.1 %collective-permute-start.1 = (bf16[16,34,192]{2,1,0:T(8,128)(2,1)S(1)}, bf16[16,34,192]{2,1,0:T(8,128)(2,1)S(1)}, u32[]{:S(2)}, u32[]{:S(2)}) collective-permute-start(bf16[16,34,192]{2,1,0:T(8,128)(2,1)S(1)} %get-tuple-element.7), channel_id=1, source_target_pairs={{8,0},{16,8},{24,16},{0,24},{9,1},{17,9},{25,17},{1,25},{10,2},{18... | collective-permute-start | bytes 626696 | tf_op jit(solution)/shard_map/ppermute | solution.py:17
  7.3 0.0 collective-permute-start
  7.3 0.0 copy-done.6
  7.3 0.6 fusion.3
  9.0 0.2 fusion
  9.2 0.1 copy.23
  9.3 0.1 copy.24
  9.3 0.0 copy-done
  9.4 30.8 %all_gather.6.down_weight_ref = bf16[768,384]{1,0:T(8,128)(2,1)} all-gather(bf16[48,384]{1,0:T(8,128)(2,1)S(1)} %copy-done), channel_id=1, replica_groups=mesh['lon'=4,'lat'=4,'mem'=2] {'lon','lat'}, dimensions={0}, use_global_device_ids=true | all-gather | bytes 626688 | tf_op jit(solution)/shard_map/all_gather | solution.py:201
  40.2 0.0 collective-permute-done.1.east_ref
  40.2 0.0 copy-start.4
  40.2 0.0 collective-permute-done.west_ref
  40.2 0.0 copy-start.5
  40.3 0.1 pad_maximum_fusion.1
  40.3 1.3 %collective-permute-start.3 = (bf16[16,8,192]{2,1,0:T(8,128)(2,1)S(1)}, bf16[16,8,192]{2,1,0:T(8,128)(2,1)S(1)}, u32[]{:S(2)}, u32[]{:S(2)}) collective-permute-start(bf16[16,8,192]{2,1,0:T(8,128)(2,1)S(1)} %pad_maximum_fusion.1), channel_id=1, source_target_pairs={{2,0},{4,2},{6,4},{3,1},{5,3},{7,5},{10,8},{12,10},{14,12},{11,9},... | collective-permute-start | bytes 147464 | tf_op jit(solution)/shard_map/ppermute | solution.py:23
  41.6 0.1 pad_maximum_fusion
  41.7 3.0 %collective-permute-start.2 = (bf16[16,8,192]{2,1,0:T(8,128)(2,1)S(1)}, bf16[16,8,192]{2,1,0:T(8,128)(2,1)S(1)}, u32[]{:S(2)}, u32[]{:S(2)}) collective-permute-start(bf16[16,8,192]{2,1,0:T(8,128)(2,1)S(1)} %pad_maximum_fusion), channel_id=1, source_target_pairs={{0,2},{2,4},{4,6},{1,3},{3,5},{5,7},{8,10},{10,12},{12,14},{9,11},... | collective-permute-start | bytes 147464 | tf_op jit(solution)/shard_map/ppermute | solution.py:23
  44.8 0.0 copy-done.1
  44.8 21.7 %all_gather.7.up_weight_ref = bf16[384,768]{1,0:T(8,128)(2,1)} all-gather(bf16[24,768]{1,0:T(8,128)(2,1)S(1)} %copy-done.1), channel_id=1, replica_groups=mesh['lon'=4,'lat'=4,'mem'=2] {'lon','lat'}, dimensions={0}, use_global_device_ids=true | all-gather | bytes 626688 | tf_op jit(solution)/shard_map/all_gather | solution.py:202
  66.5 0.0 copy-start.2
  66.5 0.0 copy-start.3
  66.5 2.4 %copy.17.tokens_ref = bf16[16,34,6,192]{3,2,1,0:T(8,128)(2,1)} copy(bf16[16,34,6,192]{3,1,0,2:T(8,128)(2,1)S(1)} %bitcast.18) | data formatting | bytes 2506752 | tf_op jit(solution)/shard_map/reshape | solution.py:190
  68.8 0.0 copy-done.4
  68.8 0.0 copy-done.5
  68.8 0.0 copy-done.2
  68.8 0.7 reshape.24.down_gain_ref
  69.5 0.0 copy-done.3
  69.5 0.6 reshape.25.down_shift_ref
  70.1 0.0 collective-permute-done.3.south_ref
  70.2 0.0 copy-start.7
  70.2 0.0 collective-permute-done.2.north_ref
  70.2 0.0 copy-start.8
  70.2 0.6 copy-done.7
  70.8 0.0 copy-done.8
  70.8 17.3 %shard_map.91 = bf16[16,34,6,192]{3,2,1,0:T(8,128)(2,1)} custom-call(s32[1,2]{1,0:T(1,128)} %band_ref.1, bf16[16,34,6,192]{3,2,1,0:T(8,128)(2,1)} %copy.17.tokens_ref, bf16[16,34,192]{2,1,0:T(8,128)(2,1)} %copy-done.5, bf16[16,34,192]{2,1,0:T(8,128)(2,1)} %copy-done.4, bf16[16,8,192]{2,1,0:T(8,128)(2,1)} %copy-done.8, bf16[16,8,192]{2,1,0:T(8,128)(2,1)} %copy-done.7, ...), custom_call_target="tpu_custom_call" | custom-call | flops 3000000000 | bytes 8000000 | tf_op jit(solution)/shard_map/pallas_call | solution.py:158
  88.1 3.7 %copy.18 = bf16[2,8,34,6,192]{4,1,3,2,0:T(8,128)(2,1)} copy(bf16[2,8,34,6,192]{4,3,2,1,0:T(8,128)(2,1)} %bitcast.19) | data formatting | bytes 2506752 | tf_op jit(solution)/shard_map/reshape | solution.py:207
  (3 shorter events, 0.1 us)
Async XLA Ops:
  0.0 7.3 %copy-start.6 = (s32[1,2]{1,0:T(1,128)S(1)}, s32[1,2]{1,0:T(1,128)}, u32[]{:S(2)}) copy-start(s32[1,2]{1,0:T(1,128)} %band_ref.1) | copy-start | bytes 28
  0.0 9.3 %copy-start = (bf16[48,384]{1,0:T(8,128)(2,1)S(1)}, bf16[48,384]{1,0:T(8,128)(2,1)}, u32[]{:S(2)}) copy-start(bf16[48,384]{1,0:T(8,128)(2,1)} %param.13) | copy-start | bytes 110596
  2.1 42.7 %copy-start.1 = (bf16[24,768]{1,0:T(8,128)(2,1)S(1)}, bf16[24,768]{1,0:T(8,128)(2,1)}, u32[]{:S(2)}) copy-start(bf16[24,768]{1,0:T(8,128)(2,1)} %param.14) | copy-start | bytes 110596
  2.1 38.0 %collective-permute-start.1 = (bf16[16,34,192]{2,1,0:T(8,128)(2,1)S(1)}, bf16[16,34,192]{2,1,0:T(8,128)(2,1)S(1)}, u32[]{:S(2)}, u32[]{:S(2)}) collective-permute-start(bf16[16,34,192]{2,1,0:T(8,128)(2,1)S(1)} %get-tuple-element.7), channel_id=1, source_target_pairs={{8,0},{16,8},{24,16},{0,24},{9,1},{17,9},{25,17},{1,25},{10,2},{18... | collective-permute-start | bytes 626696 | tf_op jit(solution)/shard_map/ppermute | solution.py:17
  7.3 32.9 %collective-permute-start = (bf16[16,34,192]{2,1,0:T(8,128)(2,1)S(1)}, bf16[16,34,192]{2,1,0:T(8,128)(2,1)S(1)}, u32[]{:S(2)}, u32[]{:S(2)}) collective-permute-start(bf16[16,34,192]{2,1,0:T(8,128)(2,1)S(1)} %get-tuple-element.8), channel_id=1, source_target_pairs={{24,0},{0,8},{8,16},{16,24},{25,1},{1,9},{9,17},{17,25},{26,2},{2,... | collective-permute-start | bytes 626696 | tf_op jit(solution)/shard_map/ppermute | solution.py:17
  40.2 28.6 %copy-start.4 = (bf16[16,34,192]{2,1,0:T(8,128)(2,1)}, bf16[16,34,192]{2,1,0:T(8,128)(2,1)S(1)}, u32[]{:S(2)}) copy-start(bf16[16,34,192]{2,1,0:T(8,128)(2,1)S(1)} %collective-permute-done.1.east_ref) | copy-start | bytes 626692
  40.2 28.6 %copy-start.5 = (bf16[16,34,192]{2,1,0:T(8,128)(2,1)}, bf16[16,34,192]{2,1,0:T(8,128)(2,1)S(1)}, u32[]{:S(2)}) copy-start(bf16[16,34,192]{2,1,0:T(8,128)(2,1)S(1)} %collective-permute-done.west_ref) | copy-start | bytes 626692
  40.3 29.8 %collective-permute-start.3 = (bf16[16,8,192]{2,1,0:T(8,128)(2,1)S(1)}, bf16[16,8,192]{2,1,0:T(8,128)(2,1)S(1)}, u32[]{:S(2)}, u32[]{:S(2)}) collective-permute-start(bf16[16,8,192]{2,1,0:T(8,128)(2,1)S(1)} %pad_maximum_fusion.1), channel_id=1, source_target_pairs={{2,0},{4,2},{6,4},{3,1},{5,3},{7,5},{10,8},{12,10},{14,12},{11,9},... | collective-permute-start | bytes 147464 | tf_op jit(solution)/shard_map/ppermute | solution.py:23
  41.7 28.4 %collective-permute-start.2 = (bf16[16,8,192]{2,1,0:T(8,128)(2,1)S(1)}, bf16[16,8,192]{2,1,0:T(8,128)(2,1)S(1)}, u32[]{:S(2)}, u32[]{:S(2)}) collective-permute-start(bf16[16,8,192]{2,1,0:T(8,128)(2,1)S(1)} %pad_maximum_fusion), channel_id=1, source_target_pairs={{0,2},{2,4},{4,6},{1,3},{3,5},{5,7},{8,10},{10,12},{12,14},{9,11},... | collective-permute-start | bytes 147464 | tf_op jit(solution)/shard_map/ppermute | solution.py:23
  66.5 2.4 %copy-start.2 = (f32[768]{0:T(1024)S(1)}, f32[768]{0:T(1024)}, u32[]{:S(2)}) copy-start(f32[768]{0:T(1024)} %param.11) | copy-start | bytes 9220
  66.5 3.0 %copy-start.3 = (f32[768]{0:T(1024)S(1)}, f32[768]{0:T(1024)}, u32[]{:S(2)}) copy-start(f32[768]{0:T(1024)} %param.12) | copy-start | bytes 9220
  70.2 0.6 copy-start.7
  70.2 0.6 copy-start.8

commit v2 on v0

v2 whole, which is shorter than its diff:
```python
import functools

import jax
import jax.numpy as jnp
from jax import lax
from jax.experimental import pallas as pl
from jax.experimental.pallas import tpu as pltpu
from jax.sharding import PartitionSpec as P

MESH = pl.DeviceIdType.MESH


def normalized(planes, gains, shifts, width):
    total = functools.reduce(jnp.add, planes)
    average = jnp.sum(total, axis=-1, keepdims=True) * (1.0 / width)
    centred = [plane - average for plane in planes]
    squares = functools.reduce(jnp.add, [c * c for c in centred])
    spread = jnp.sum(squares, axis=-1, keepdims=True) * (1.0 / width)
    scale = lax.rsqrt(spread + 1e-05)
    return [
        (c * scale * gain + shift).astype(jnp.bfloat16)
        for c, gain, shift in zip(centred, gains, shifts)
    ]


def kernel(
    sizes, band_ref, tokens_ref, shards_ref, down_gain_ref, down_shift_ref,
    up_gain_ref, up_shift_ref, mix_ref, out_ref,
    held, west, east, north, south, last, gathered, down_wide, up_wide, down_all, up_all,
    merged, results,
    local_sem, send_lon, recv_lon, send_plane, recv_plane, send_twin, recv_twin,
    send_side, recv_side,
):
    n_lon, n_lat, n_mem = sizes
    members, slots, columns, levels, features = held.shape
    kinds, _, _, shard_rows, shard_cols = gathered.shape
    half_rows = slots // 2 + 1
    half_cols = columns // 2 + 1
    lon, lat, mem = lax.axis_index("lon"), lax.axis_index("lat"), lax.axis_index("mem")
    twin = lat + 1 - 2 * lax.rem(lat, 2)
    first_row = band_ref[0, 0]
    live = band_ref[0, 1] - first_row
    odd = lax.rem(first_row, 2)

    def wrap(value, size):
        return lax.rem(value + size, size)

    def at(d_lon=0, d_lat=0, d_mem=0):
        return (wrap(lon + d_lon, n_lon), wrap(lat + d_lat, n_lat), wrap(mem + d_mem, n_mem))

    peers = [(dx, dm) for dx in range(n_lat // 2) for dm in range(n_mem) if (dx, dm) != (0, 0)]
    around = [(a, b) for a in (-1, 0, 1) for b in (-1, 0, 1) if (a, b) != (0, 0)]

    own_tokens = pltpu.make_async_copy(tokens_ref, held, local_sem.at[0])
    own_tokens.start()
    own_shard = pltpu.make_async_copy(
        shards_ref.at[mem], gathered.at[mem, lon, lat], local_sem.at[1]
    )
    own_shard.start()

    barrier = pltpu.get_barrier_semaphore()
    others = [at(d) for d in range(1, n_lon)]
    others += [at(0, 2 * dx, dm) for dx, dm in peers]
    others += [(lon, twin, mem)]
    others += [at(a, b) for a, b in around]
    for other in others:
        pl.semaphore_signal(barrier, inc=1, device_id=other, device_id_type=MESH)

    own_tokens.wait()
    last[...] = held[:, jnp.clip(live - 1, 0, slots - 1)]
    own_shard.wait()
    pl.semaphore_wait(barrier, len(others))

    started = []

    def send(source, target, send_sem, recv_sem, device):
        copy = pltpu.make_async_remote_copy(
            src_ref=source, dst_ref=target, send_sem=send_sem, recv_sem=recv_sem,
            device_id=device, device_id_type=MESH,
        )
        copy.start()
        started.append(copy)

    def arrived(target, send_sem, recv_sem, device):
        pltpu.make_async_remote_copy(
            src_ref=target, dst_ref=target, send_sem=send_sem, recv_sem=recv_sem,
            device_id=device, device_id_type=MESH,
        ).wait_recv()

    mine = gathered.at[mem, lon, lat]
    for d in range(1, n_lon):
        send(mine, mine, send_lon.at[d], recv_lon.at[d], at(d))

    sides = []
    for index, (a, b) in enumerate(around):
        column = {-1: 0, 1: columns - 1}.get(a)
        slot = {-1: columns + 1, 1: 0}.get(a)
        if b == 0:
            source, target = held.at[:, :, column], (east if a < 0 else west)
        else:
            row = last if b > 0 else held.at[:, 0]
            place = north if b > 0 else south
            if a == 0:
                source, target = row, place.at[:, pl.ds(1, columns)]
                if b < 0:
                    source = held.at[:, 0]
            else:
                source = last.at[:, column] if b > 0 else held.at[:, 0, column]
                target = place.at[:, slot]
        send(source, target, send_side.at[index], recv_side.at[index], at(a, b))
        sides.append((target, index, at(-a, -b)))

    def to_plane(d):
        chunk = gathered.at[mem, wrap(lon - d, n_lon), lat]
        for k, (dx, dm) in enumerate(peers):
            send(chunk, chunk, send_plane.at[k, d], recv_plane.at[k, d], at(0, 2 * dx, dm))
        send(chunk, chunk, send_twin.at[0, d], recv_twin.at[0, d], (lon, twin, mem))

    to_plane(0)
    for d in range(1, n_lon):
        chunk = gathered.at[mem, wrap(lon - d, n_lon), lat]
        arrived(chunk, send_lon.at[d], recv_lon.at[d], at(-d))
        to_plane(d)

    for target, index, device in sides:
        arrived(target, send_side.at[index], recv_side.at[index], device)

    bottom = lat == n_lat - 1
    chunk_rows = max(r for r in range(1, 10) if half_rows % r == 0)
    chunks = half_rows // chunk_rows
    rows_each = chunk_rows * half_cols * levels
    gains = [down_gain_ref[i : i + 1] for i in range(4)]
    shifts = [down_shift_ref[i : i + 1] for i in range(4)]
    order = [(p, q) for q in range(2) for p in range(2)]

    def merge(step, carry):
        member, begin = step // chunks, lax.rem(step, chunks) * chunk_rows
        planes = {pq: [] for pq in order}
        for k in range(chunk_rows):
            for p in range(2):
                row = 2 * (begin + k) + p - odd
                safe = jnp.clip(row, 0, slots - 1)
                for c in range(columns + 2):
                    if c == 0:
                        cell = west[member, safe]
                    elif c == columns + 1:
                        cell = east[member, safe]
                    else:
                        cell = held[member, safe, c - 1]
                    cell = cell.astype(jnp.float32)
                    below = south[member, c].astype(jnp.float32)
                    below = jnp.where(bottom, jnp.zeros_like(below), below)
                    cell = jnp.where(row == live, below, cell)
                    if k == 0 and p == 0:
                        cell = jnp.where(row < 0, north[member, c].astype(jnp.float32), cell)
                    planes[p, c % 2].append(cell)
        parts = normalized(
            [jnp.concatenate(planes[pq], 0) for pq in order], gains, shifts, 4 * features
        )
        for i, part in enumerate(parts):
            merged[i, step] = part
        return carry

    lax.fori_loop(0, members * chunks, merge, 0)

    for d in range(n_lon):
        for k, (dx, dm) in enumerate(peers):
            chunk = gathered.at[
                wrap(mem - dm, n_mem), wrap(lon - d, n_lon), wrap(lat - 2 * dx, n_lat)
            ]
            arrived(chunk, send_plane.at[k, d], recv_plane.at[k, d], at(0, -2 * dx, -dm))
            send(
                chunk, chunk, send_twin.at[k + 1, d], recv_twin.at[k + 1, d], (lon, twin, mem)
            )
    for d in range(n_lon):
        for k, (dx, dm) in enumerate([(0, 0)] + peers):
            chunk = gathered.at[
                wrap(mem - dm, n_mem), wrap(lon - d, n_lon), wrap(twin - 2 * dx, n_lat)
            ]
            arrived(chunk, send_twin.at[k, d], recv_twin.at[k, d], (lon, twin, mem))

    half = shard_rows // 2
    for l in range(n_lon):
        for t in range(n_lat):
            place = l * n_lat + t
            down_wide[pl.ds(place * shard_rows, shard_rows), :] = gathered[0, l, t].astype(
                jnp.float32
            )
            block = gathered[1, l, t].astype(jnp.float32)
            for p in range(2):
                piece = block[p * half : (p + 1) * half]
                for q in range(2):
                    up_wide[2 * p + q, pl.ds(place * half, half), :] = piece[
                        :, q * features : (q + 1) * features
                    ]
    down_all[...] = down_wide[...].astype(jnp.bfloat16)
    for i in range(4):
        up_all[i] = up_wide[i].astype(jnp.bfloat16)

    def expand(step, carry):
        member, begin = step // chunks, lax.rem(step, chunks) * chunk_rows
        coarse = functools.reduce(
            jnp.add,
            [
                jnp.dot(
                    merged[i, step], down_all[i * features : (i + 1) * features],
                    preferred_element_type=jnp.float32,
                )
                for i in range(4)
            ],
        ).astype(jnp.bfloat16)
        for p in range(2):
            for q in range(2):
                grown = jnp.dot(coarse, up_all[2 * p + q], preferred_element_type=jnp.float32)
                (fine,) = normalized([grown], [up_gain_ref[...]], [up_shift_ref[...]], features)
                fine = jnp.dot(fine, mix_ref[...], preferred_element_type=jnp.float32)
                fine = fine.reshape(chunk_rows, half_cols, levels, features)
                for k in range(chunk_rows):
                    for j in range(half_cols):
                        column = 2 * j + q - 1
                        if 0 <= column < columns:
                            results[member, 2 * (begin + k) + p, column] = fine[k, j]
        return carry

    lax.fori_loop(0, members * chunks, expand, 0)

    def finish(row, carry):
        for member in range(members):
            values = results[member, row + odd]
            values = jnp.where(row < live, values, jnp.zeros_like(values))
            out_ref[member, row] = values.astype(jnp.bfloat16)
        return carry

    lax.fori_loop(0, slots, finish, 0)
    for copy in started:
        copy.wait_send()


def body(
    sizes, tokens, band_rows, down_gain, down_shift, down_weight, up_weight, up_gain, up_shift,
    mix_weight,
):
    n_lon, n_lat, n_mem = sizes
    members, levels, slots, columns, features = tokens.shape
    cells = tokens.transpose(0, 2, 3, 1, 4)
    up_rows, up_cols = up_weight.shape
    shard_rows, shard_cols = down_weight.shape
    up_folded = up_weight.reshape(up_rows, 2, up_cols // 2).transpose(1, 0, 2)
    shards = jnp.stack([down_weight, up_folded.reshape(shard_rows, shard_cols)])
    half_rows, half_cols = slots // 2 + 1, columns // 2 + 1
    chunk_rows = max(r for r in range(1, 10) if half_rows % r == 0)
    steps = members * half_rows // chunk_rows
    n_peers = n_lat // 2 * n_mem - 1
    n_all = n_lon * n_lat
    bf16, f32 = jnp.bfloat16, jnp.float32
    vmem = pl.BlockSpec(memory_space=pltpu.VMEM)
    dma = pltpu.SemaphoreType.DMA
    out = pl.pallas_call(
        functools.partial(kernel, sizes),
        out_shape=jax.ShapeDtypeStruct(cells.shape, cells.dtype),
        in_specs=[
            pl.BlockSpec(memory_space=pltpu.SMEM), pl.BlockSpec(memory_space=pl.ANY),
            vmem, vmem, vmem, vmem, vmem, vmem,
        ],
        out_specs=vmem,
        scratch_shapes=[
            pltpu.VMEM(cells.shape, bf16),
            pltpu.VMEM((members, slots, levels, features), bf16),
            pltpu.VMEM((members, slots, levels, features), bf16),
            pltpu.VMEM((members, columns + 2, levels, features), bf16),
            pltpu.VMEM((members, columns + 2, levels, features), bf16),
            pltpu.VMEM((members, columns, levels, features), bf16),
            pltpu.VMEM((2, n_lon, n_lat, shard_rows, shard_cols), bf16),
            pltpu.VMEM((n_all * shard_rows, shard_cols), f32),
            pltpu.VMEM((4, n_all * up_rows, features), f32),
            pltpu.VMEM((n_all * shard_rows, shard_cols), bf16),
            pltpu.VMEM((4, n_all * up_rows, features), bf16),
            pltpu.VMEM((4, steps, chunk_rows * half_cols * levels, features), bf16),
            pltpu.VMEM((members, 2 * half_rows, columns, levels, features), f32),
            dma((2,)),
            dma((n_lon,)), dma((n_lon,)),
            dma((n_peers, n_lon)), dma((n_peers, n_lon)),
            dma((n_peers + 1, n_lon)), dma((n_peers + 1, n_lon)),
            dma((8,)), dma((8,)),
        ],
        compiler_params=pltpu.CompilerParams(collective_id=0, has_side_effects=True),
        cost_estimate=pl.CostEstimate(
            flops=3_000_000_000, bytes_accessed=8_000_000, transcendentals=0
        ),
    )(
        band_rows, cells, shards, down_gain.reshape(4, features), down_shift.reshape(4, features),
        up_gain.reshape(1, features), up_shift.reshape(1, features), mix_weight,
    )
    return out.transpose(0, 3, 1, 2, 4)


def solution(mesh):
    sizes = tuple(mesh.shape[name] for name in ("lon", "lat", "mem"))
    assert sizes[2] == 2
    return jax.shard_map(
        functools.partial(body, sizes),
        mesh=mesh,
        in_specs=(
            P("mem", None, "lat", "lon", None),
            P("lat", None),
            P(),
            P(),
            P(("lon", "lat"), None),
            P(("lon", "lat"), None),
            P(),
            P(),
            P(),
        ),
        out_specs=P("mem", None, "lat", "lon", None),
        check_vma=False,
    )
```

time: 136 us -> 47.6 us (0.35)
  blocking collectives: 43.4 us -> 0 us
  Pallas kernels: 0 us -> 39.6 us
  local copies, waits for them, and re-layouts: 38.6 us -> 6.2 us
  other arithmetic: 19.2 us -> 1.41 us
  waiting for transfers between devices: 11.8 us -> 0 us
  starting transfers between devices: 11 us -> 0 us
  matrix products: 7.64 us -> 0 us
  between operations: 3.41 us -> 0.01 us
    all_gather x2 -> x0, blocking collectives: 43.4 us -> none  [the longest x1 22.9 us: body(): lax.all_gather(down_weight, ('lon', 'lat'), axis=0, tiled=True)]
    pallas_call x0 -> x1, Pallas kernels: none -> 39.6 us  [body(): pl.pallas_call(functools.partial(kernel, sizes), out_shape=jax.ShapeDtype...]
    reshape x5 -> x3, local copies, waits for them, and re-layouts: 19.4 us -> 3.48 us  [the longest x1 1.35 us: body(): down_gain.reshape(4, features)]
    convert_element_type x3 -> x0, local copies, waits for them, and re-layouts: 13.6 us -> none  [the longest x2 11.4 us: body(): merged.astype(jnp.float32)]
    ppermute x4 -> x0, waiting for transfers between devices: 11.8 us -> none  [the longest x2 10.3 us: shifted(): return lax.ppermute(block, axis, route)]
    reduce_sum x4 -> x0, other arithmetic: 11.3 us -> none  [the longest x2 6.61 us: normalize(): spread = jnp.mean(centred * centred, axis=-1, keepdims=True)]
    ppermute x4 -> x0, starting transfers between devices: 11 us -> none  [the longest x2 5.84 us: passed_along(): return lax.ppermute(block, axis, route)]
    dot_general x2 -> x0, matrix products: 7.64 us -> none  [the longest x1 4.37 us: body(): jnp.dot(columns_used, lax.all_gather(up_weight, ('lon', 'lat'), axis=0, t...]
  transfers between devices with their start and end apart: 4 -> 0, of which waited for: 2 -> 0; matrix products, arithmetic and copies ran while one was open for 2% -> 0% of each run, Pallas kernels for 0% -> 0%
where the time goes in v2:
time: 47.6 us; the launch traced here: 47.2 us
  Pallas kernels  39.6 us (83%)
  local copies, waits for them, and re-layouts  6.2 us (13%)
  other arithmetic  1.41 us (3%)
    pallas_call x1, Pallas kernels, body(): pl.pallas_call(functools.partial(kernel, sizes), out_shape=jax.ShapeDtype...  39.6 us
    unnamed x1, local copies, waits for them, and re-layouts  2.72 us
    another operation x1, other arithmetic, body(): shards = jnp.stack([down_weight, up_folded.reshape(shard_rows, shard_cols)])  1.41 us
    reshape x1, local copies, waits for them, and re-layouts, body(): down_gain.reshape(4, features)  1.35 us
    reshape x1, local copies, waits for them, and re-layouts, body(): down_shift.reshape(4, features)  1.35 us

profile of v2, /device:TPU:0, one launch (start us, length us, event | category | flops | bytes accessed | tf_op | source)
XLA Modules:
  0.0 47.2 jit_solution(12292241777772432128)
XLA Ops:
  0.0 1.4 %reshape.16.down_gain_ref = f32[4,192]{1,0:T(4,128)} reshape(f32[768]{0:T(1024)} %param.11) | data formatting | bytes 6144 | tf_op jit(solution)/shard_map/reshape | solution.py:291
  1.4 1.4 %reshape.17.down_shift_ref = f32[4,192]{1,0:T(4,128)} reshape(f32[768]{0:T(1024)} %param.12) | data formatting | bytes 6144 | tf_op jit(solution)/shard_map/reshape | solution.py:291
  2.7 0.8 %copy.13 = bf16[3,2,8,384]{3,2,0,1:T(8,128)(2,1)S(1)} copy(bf16[3,2,8,384]{3,2,1,0:T(8,128)(2,1)} %bitcast.14) | data formatting | bytes 73728 | tf_op jit(solution)/shard_map/reshape | solution.py:248
  3.5 1.4 %pad_maximum_fusion.shards_ref = bf16[2,48,384]{2,1,0:T(8,128)(2,1)} fusion(bf16[1,48,384]{2,1,0:T(8,128)(2,1)S(1)} %bitcast.13, bf16[1,48,384]{2,1,0:T(8,128)(2,1)} %bitcast.15), kind=kLoop, calls=%fused_computation | loop fusion | flops 36864 | bytes 147456 | tf_op jit(solution)/shard_map/stack | solution.py:249
  4.9 39.6 %shard_map.91 = bf16[2,34,6,8,192]{4,3,2,1,0:T(8,128)(2,1)} custom-call(s32[1,2]{1,0:T(1,128)} %band_ref.1, bf16[2,34,6,8,192]{4,3,2,1,0:T(8,128)(2,1)} %bitcast.16, bf16[2,48,384]{2,1,0:T(8,128)(2,1)} %pad_maximum_fusion.shards_ref, f32[4,192]{1,0:T(4,128)} %reshape.16.down_gain_ref, f32[4,192]{1,0:T(4,128)} %reshape.17.down_shift_ref, f32[1,192]{1,0:T(1,128)} %bitcast.17, ...), custom_call_target="tpu_custom_call" | custom-call | flops 3000000000 | bytes 8000000 | tf_op jit(solution)/shard_map/pallas_call | solution.py:258
  44.5 2.7 %copy.15 = bf16[2,8,34,6,192]{4,1,3,2,0:T(8,128)(2,1)} copy(bf16[2,8,34,6,192]{4,1,3,2,0:T(8,128)(2,1)} %bitcast.12) | data formatting | bytes 2506752

commit v3 on v2

--- a/solution.py
+++ b/solution.py
@@ -1,4 +1,5 @@
 import functools
+import math
 
 import jax
 import jax.numpy as jnp
@@ -24,16 +25,17 @@
 
 
 def kernel(
-    sizes, band_ref, tokens_ref, shards_ref, down_gain_ref, down_shift_ref,
+    sizes, band_ref, tokens_ref, down_ref, up_ref, down_gain_ref, down_shift_ref,
     up_gain_ref, up_shift_ref, mix_ref, out_ref,
-    held, west, east, north, south, last, gathered, down_wide, up_wide, down_all, up_all,
+    held, west, east, to_west, to_east, north, south, last, gathered, down_wide, up_wide, down_all, up_all,
     merged, results,
     local_sem, send_lon, recv_lon, send_plane, recv_plane, send_twin, recv_twin,
     send_side, recv_side,
 ):
     n_lon, n_lat, n_mem = sizes
     members, slots, columns, levels, features = held.shape
-    kinds, _, _, shard_rows, shard_cols = gathered.shape
+    _, _, _, shard_blocks, block_rows, shard_cols = gathered.shape
+    shard_rows = shard_blocks * block_rows
     half_rows = slots // 2 + 1
     half_cols = columns // 2 + 1
     lon, lat, mem = lax.axis_index("lon"), lax.axis_index("lat"), lax.axis_index("mem")
@@ -49,14 +51,29 @@
         return (wrap(lon + d_lon, n_lon), wrap(lat + d_lat, n_lat), wrap(mem + d_mem, n_mem))
 
     peers = [(dx, dm) for dx in range(n_lat // 2) for dm in range(n_mem) if (dx, dm) != (0, 0)]
-    around = [(a, b) for a in (-1, 0, 1) for b in (-1, 0, 1) if (a, b) != (0, 0)]
+    around = [(0, 1), (0, -1), (1, 1), (1, -1), (-1, 1), (-1, -1), (1, 0), (-1, 0)]
 
     own_tokens = pltpu.make_async_copy(tokens_ref, held, local_sem.at[0])
     own_tokens.start()
-    own_shard = pltpu.make_async_copy(
-        shards_ref.at[mem], gathered.at[mem, lon, lat], local_sem.at[1]
-    )
-    own_shard.start()
+    half_blocks = shard_blocks // 2
+    down_copy = pltpu.make_async_copy(down_ref, gathered.at[0, lon, lat], local_sem.at[1])
+    up_copies = [
+        pltpu.make_async_copy(
+            up_ref.at[:, :, pl.ds(p * shard_cols, shard_cols)],
+            gathered.at[1, lon, lat, pl.ds(p * half_blocks, half_blocks)],
+            local_sem.at[2 + p],
+        )
+        for p in range(2)
+    ]
+
+    @pl.when(mem == 0)
+    def _():
+        down_copy.start()
+
+    @pl.when(mem == 1)
+    def _():
+        for copy in up_copies:
+            copy.start()
 
     barrier = pltpu.get_barrier_semaphore()
     others = [at(d) for d in range(1, n_lon)]
@@ -67,8 +84,21 @@
         pl.semaphore_signal(barrier, inc=1, device_id=other, device_id_type=MESH)
 
     own_tokens.wait()
+    for packed, column in ((to_west, 0), (to_east, columns - 1)):
+        packed[...] = jnp.concatenate(
+            [held[m, :, column].astype(jnp.float32) for m in range(members)], -1
+        ).astype(jnp.bfloat16)
     last[...] = held[:, jnp.clip(live - 1, 0, slots - 1)]
-    own_shard.wait()
+
+    @pl.when(mem == 0)
+    def _():
+        down_copy.wait()
+
+    @pl.when(mem == 1)
+    def _():
+        for copy in up_copies:
+            copy.wait()
+
     pl.semaphore_wait(barrier, len(others))
 
     started = []
@@ -96,7 +126,7 @@
         column = {-1: 0, 1: columns - 1}.get(a)
         slot = {-1: columns + 1, 1: 0}.get(a)
         if b == 0:
-            source, target = held.at[:, :, column], (east if a < 0 else west)
+            source, target = (to_west, east) if a < 0 else (to_east, west)
         else:
             row = last if b > 0 else held.at[:, 0]
             place = north if b > 0 else south
@@ -122,46 +152,84 @@
         arrived(chunk, send_lon.at[d], recv_lon.at[d], at(-d))
         to_plane(d)
 
-    for target, index, device in sides:
-        arrived(target, send_side.at[index], recv_side.at[index], device)
-
     bottom = lat == n_lat - 1
     chunk_rows = max(r for r in range(1, 10) if half_rows % r == 0)
     chunks = half_rows // chunk_rows
-    rows_each = chunk_rows * half_cols * levels
-    gains = [down_gain_ref[i : i + 1] for i in range(4)]
-    shifts = [down_shift_ref[i : i + 1] for i in range(4)]
+    gain_row = down_gain_ref[...].reshape(1, 4 * features)
+    shift_row = down_shift_ref[...].reshape(1, 4 * features)
+    gains = [gain_row[:, i * features : (i + 1) * features] for i in range(4)]
+    shifts = [shift_row[:, i * features : (i + 1) * features] for i in range(4)]
     order = [(p, q) for q in range(2) for p in range(2)]
 
-    def merge(step, carry):
-        member, begin = step // chunks, lax.rem(step, chunks) * chunk_rows
+    def merge(pairs, rows_done, step, carry):
+        begin = step * chunk_rows
         planes = {pq: [] for pq in order}
-        for k in range(chunk_rows):
-            for p in range(2):
-                row = 2 * (begin + k) + p - odd
-                safe = jnp.clip(row, 0, slots - 1)
-                for c in range(columns + 2):
-                    if c == 0:
-                        cell = west[member, safe]
-                    elif c == columns + 1:
-                        cell = east[member, safe]
-                    else:
-                        cell = held[member, safe, c - 1]
-                    cell = cell.astype(jnp.float32)
-                    below = south[member, c].astype(jnp.float32)
-                    below = jnp.where(bottom, jnp.zeros_like(below), below)
-                    cell = jnp.where(row == live, below, cell)
-                    if k == 0 and p == 0:
-                        cell = jnp.where(row < 0, north[member, c].astype(jnp.float32), cell)
-                    planes[p, c % 2].append(cell)
+        for member in range(members):
+            lanes = slice(member * features, (member + 1) * features)
+            for k in range(chunk_rows):
+                for p in range(2):
+                    row = 2 * (begin + k) + p - odd
+                    safe = jnp.clip(row, 0, slots - 1)
+                    for c in [2 * j + q for j in pairs for q in range(2)]:
+                        if c == 0:
+                            cell = west[safe][:, lanes]
+                        elif c == columns + 1:
+                            cell = east[safe][:, lanes]
+                        else:
+                            cell = held[member, safe, c - 1]
+                        cell = cell.astype(jnp.float32)
+                        below = south[member, c].astype(jnp.float32)
+                        below = jnp.where(bottom, jnp.zeros_like(below), below)
+                        cell = jnp.where(row == live, below, cell)
+                        if k == 0 and p == 0:
+                            cell = jnp.where(row < 0, north[member, c].astype(jnp.float32), cell)
+                        planes[p, c % 2].append(cell)
         parts = normalized(
             [jnp.concatenate(planes[pq], 0) for pq in order], gains, shifts, 4 * features
         )
         for i, part in enumerate(parts):
-            merged[i, step] = part
+            merged[i, rows_done + step, : part.shape[0]] = part
         return carry
 
-    lax.fori_loop(0, members * chunks, merge, 0)
+    def expand(pairs, rows_done, step, carry):
+        begin = step * chunk_rows
+        cells = members * chunk_rows * len(pairs)
+        coarse = functools.reduce(
+            jnp.add,
+            [
+                jnp.dot(
+                    merged[i, rows_done + step, : cells * levels],
+                    down_all[i * features : (i + 1) * features],
+                    preferred_element_type=jnp.float32,
+                )
+                for i in range(4)
+            ],
+        ).astype(jnp.bfloat16)
+        for p in range(2):
+            for q in range(2):
+                grown = jnp.dot(coarse, up_all[2 * p + q], preferred_element_type=jnp.float32)
+                (fine,) = normalized([grown], [up_gain_ref[...]], [up_shift_ref[...]], features)
+                fine = jnp.dot(fine, mix_ref[...], preferred_element_type=jnp.float32)
+                fine = fine.reshape(members, chunk_rows, len(pairs), levels, features)
+                for member in range(members):
+                    for k in range(chunk_rows):
+                        for at_pair, j in enumerate(pairs):
+                            column = 2 * j + q - 1
+                            if 0 <= column < columns:
+                                results[member, 2 * (begin + k) + p, column] = fine[
+                                    member, k, at_pair
+                                ].astype(jnp.bfloat16)
+        return carry
+
+    inner, edges = tuple(range(1, half_cols - 1)), (0, half_cols - 1)
+
+    def settle(which):
+        for (a, b), (target, index, device) in zip(around, sides):
+            if (a == 0) == which:
+                arrived(target, send_side.at[index], recv_side.at[index], device)
+
+    settle(True)
+    lax.fori_loop(0, chunks, functools.partial(merge, inner, 0), 0)
 
     for d in range(n_lon):
         for k, (dx, dm) in enumerate(peers):
@@ -185,8 +253,8 @@
             place = l * n_lat + t
             down_wide[pl.ds(place * shard_rows, shard_rows), :] = gathered[0, l, t].astype(
                 jnp.float32
-            )
-            block = gathered[1, l, t].astype(jnp.float32)
+            ).reshape(shard_rows, shard_cols)
+            block = gathered[1, l, t].astype(jnp.float32).reshape(shard_rows, shard_cols)
             for p in range(2):
                 piece = block[p * half : (p + 1) * half]
                 for q in range(2):
@@ -197,38 +265,16 @@
     for i in range(4):
         up_all[i] = up_wide[i].astype(jnp.bfloat16)
 
-    def expand(step, carry):
-        member, begin = step // chunks, lax.rem(step, chunks) * chunk_rows
-        coarse = functools.reduce(
-            jnp.add,
-            [
-                jnp.dot(
-                    merged[i, step], down_all[i * features : (i + 1) * features],
-                    preferred_element_type=jnp.float32,
-                )
-                for i in range(4)
-            ],
-        ).astype(jnp.bfloat16)
-        for p in range(2):
-            for q in range(2):
-                grown = jnp.dot(coarse, up_all[2 * p + q], preferred_element_type=jnp.float32)
-                (fine,) = normalized([grown], [up_gain_ref[...]], [up_shift_ref[...]], features)
-                fine = jnp.dot(fine, mix_ref[...], preferred_element_type=jnp.float32)
-                fine = fine.reshape(chunk_rows, half_cols, levels, features)
-                for k in range(chunk_rows):
-                    for j in range(half_cols):
-                        column = 2 * j + q - 1
-                        if 0 <= column < columns:
-                            results[member, 2 * (begin + k) + p, column] = fine[k, j]
-        return carry
-
-    lax.fori_loop(0, members * chunks, expand, 0)
+    lax.fori_loop(0, chunks, functools.partial(expand, inner, 0), 0)
+    settle(False)
+    lax.fori_loop(0, chunks, functools.partial(merge, edges, chunks), 0)
+    lax.fori_loop(0, chunks, functools.partial(expand, edges, chunks), 0)
 
     def finish(row, carry):
         for member in range(members):
             values = results[member, row + odd]
             values = jnp.where(row < live, values, jnp.zeros_like(values))
-            out_ref[member, row] = values.astype(jnp.bfloat16)
+            out_ref[member, row] = values
         return carry
 
     lax.fori_loop(0, slots, finish, 0)
@@ -245,11 +291,11 @@
     cells = tokens.transpose(0, 2, 3, 1, 4)
     up_rows, up_cols = up_weight.shape
     shard_rows, shard_cols = down_weight.shape
-    up_folded = up_weight.reshape(up_rows, 2, up_cols // 2).transpose(1, 0, 2)
-    shards = jnp.stack([down_weight, up_folded.reshape(shard_rows, shard_cols)])
+    block_rows = math.gcd(up_rows, 8)
     half_rows, half_cols = slots // 2 + 1, columns // 2 + 1
     chunk_rows = max(r for r in range(1, 10) if half_rows % r == 0)
-    steps = members * half_rows // chunk_rows
+    steps = 2 * half_rows // chunk_rows
+    widest = members * chunk_rows * max(2, half_cols - 2) * levels
     n_peers = n_lat // 2 * n_mem - 1
     n_all = n_lon * n_lat
     bf16, f32 = jnp.bfloat16, jnp.float32
@@ -257,27 +303,29 @@
     dma = pltpu.SemaphoreType.DMA
     out = pl.pallas_call(
         functools.partial(kernel, sizes),
-        out_shape=jax.ShapeDtypeStruct(cells.shape, cells.dtype),
+        out_shape=pltpu.VMEM(cells.shape, cells.dtype),
         in_specs=[
             pl.BlockSpec(memory_space=pltpu.SMEM), pl.BlockSpec(memory_space=pl.ANY),
-            vmem, vmem, vmem, vmem, vmem, vmem,
+            vmem, vmem, vmem, vmem, vmem, vmem, vmem,
         ],
         out_specs=vmem,
         scratch_shapes=[
             pltpu.VMEM(cells.shape, bf16),
-            pltpu.VMEM((members, slots, levels, features), bf16),
-            pltpu.VMEM((members, slots, levels, features), bf16),
+            pltpu.VMEM((slots, levels, members * features), bf16),
+            pltpu.VMEM((slots, levels, members * features), bf16),
+            pltpu.VMEM((slots, levels, members * features), bf16),
+            pltpu.VMEM((slots, levels, members * features), bf16),
             pltpu.VMEM((members, columns + 2, levels, features), bf16),
             pltpu.VMEM((members, columns + 2, levels, features), bf16),
             pltpu.VMEM((members, columns, levels, features), bf16),
-            pltpu.VMEM((2, n_lon, n_lat, shard_rows, shard_cols), bf16),
+            pltpu.VMEM((2, n_lon, n_lat, shard_rows // block_rows, block_rows, shard_cols), bf16),
             pltpu.VMEM((n_all * shard_rows, shard_cols), f32),
             pltpu.VMEM((4, n_all * up_rows, features), f32),
             pltpu.VMEM((n_all * shard_rows, shard_cols), bf16),
             pltpu.VMEM((4, n_all * up_rows, features), bf16),
-            pltpu.VMEM((4, steps, chunk_rows * half_cols * levels, features), bf16),
-            pltpu.VMEM((members, 2 * half_rows, columns, levels, features), f32),
-            dma((2,)),
+            pltpu.VMEM((4, steps, widest, features), bf16),
+            pltpu.VMEM((members, 2 * half_rows, columns, levels, features), bf16),
+            dma((4,)),
             dma((n_lon,)), dma((n_lon,)),
             dma((n_peers, n_lon)), dma((n_peers, n_lon)),
             dma((n_peers + 1, n_lon)), dma((n_peers + 1, n_lon)),
@@ -288,7 +336,8 @@
             flops=3_000_000_000, bytes_accessed=8_000_000, transcendentals=0
         ),
     )(
-        band_rows, cells, shards, down_gain.reshape(4, features), down_shift.reshape(4, features),
+        band_rows, cells, down_weight.reshape(-1, block_rows, shard_cols),
+        up_weight.reshape(-1, block_rows, up_cols), down_gain, down_shift,
         up_gain.reshape(1, features), up_shift.reshape(1, features), mix_weight,
     )
     return out.transpose(0, 3, 1, 2, 4)

time: 47.6 us -> 33.1 us (0.70)
  the two profiles are of different devices: /device:TPU:0 before, /device:TPU:9 now
where the time goes in v3:
time: 33.1 us; the launch traced here: 32.9 us
  Pallas kernels  31.7 us (96%)
  local copies, waits for them, and re-layouts  1.18 us (4%)
    pallas_call x1, Pallas kernels, body(): pl.pallas_call(functools.partial(kernel, sizes), out_shape=pltpu.VMEM(cel...  31.7 us
    unnamed x1, local copies, waits for them, and re-layouts  1.18 us

profile of v3, /device:TPU:9, one launch (start us, length us, event | category | flops | bytes accessed | tf_op | source)
XLA Modules:
  0.0 32.9 jit_solution(5791036033932761609)
XLA Ops:
  0.0 31.7 %shard_map.91 = bf16[2,34,6,8,192]{4,3,2,1,0:T(8,128)(2,1)S(1)} custom-call(s32[1,2]{1,0:T(1,128)} %band_ref.1, bf16[2,34,6,8,192]{4,3,2,1,0:T(8,128)(2,1)} %bitcast.7, bf16[6,8,384]{2,1,0:T(8,128)(2,1)} %bitcast.8, bf16[3,8,768]{2,1,0:T(8,128)(2,1)} %bitcast.9, f32[768]{0:T(1024)} %down_gain_ref.1, f32[768]{0:T(1024)} %down_shift_ref.1, f32[1,192]{1,0:T(1,128)} %bitcast.10, ...), custom_call_target="tpu_custom_call" | custom-call | flops 3000000000 | bytes 8000000 | tf_op jit(solution)/shard_map/pallas_call | solution.py:304
  31.8 1.2 %copy.11 = bf16[2,8,34,6,192]{4,1,3,2,0:T(8,128)(2,1)} copy(bf16[2,8,34,6,192]{4,1,3,2,0:T(8,128)(2,1)S(1)} %bitcast.6) | data formatting | bytes 2506752
